TPU v7x, 32 devices: a whole 2x2x4 slice. The times are simulated.
32 devices in a mesh: row: 8 (over y, x, core), col: 4 (over z).
Axes of the slice: x: 2, y: 2, z: 4, core: 2. Of those that a mesh axis runs over, the one named last changes fastest.
Arguments:
- state: float32 [2048, 4, 1024], P('row', 'col'), may hold values from -6 to 6
- coupling: bfloat16 [2048, 4, 1024], P('row', 'col'), may hold values from -2 to 2, as said below
- coupling_t: bfloat16 [2, 2048, 4, 1024], P(None, 'row', 'col'), may hold values from -2 to 2, as said below
- factor: float32 [4, 4, 256, 256], P(None, 'col', 'row'), may hold values from -0.3 to 1.3
- cofactor: float32 [4, 4, 256, 256], P(None, 'col', 'row'), may hold values from -0.3 to 1.3
- rates: float32 [4, 4, 256], P(None, 'col'), may hold values from 0.5 to 2
Outputs:
- updated_state: float32 [2048, 4, 1024], P('row', 'col')
Inputs may be any that keep to these rules, and one draw needn't show every extreme that they name: coupling and coupling_t hold the same matrix A; its blocks A(i, k) are zero unless k > i. coupling_t holds the transposed blocks of the A in coupling.
All inputs are finite; a program needn't handle non-finite values.
Results may differ from a plain program's by a relative error of at most 0.0003.
Values may be sent and summed in bfloat16 or wider, within the bound.
A program may use at most 64 MiB of HBM per device.

v0:
```python
import jax
import jax.numpy as jnp
from jax import lax
from jax.sharding import PartitionSpec as P

STEPS = 2
HIGHEST_PRECISION = lax.Precision.HIGHEST


def broadcast(block, axis, source):
    block = jnp.where(lax.axis_index(axis) == source, block, jnp.zeros_like(block))
    return lax.psum(block, axis)


def from_behind(block, axis, distance):
    devices = range(lax.axis_size(axis))
    route = [((i - distance) % len(devices), i) for i in devices]
    return lax.ppermute(block, axis, route)


def solve_block(residual, left_p, left_q, left_e, right_p, right_q, right_e):
    middle = jnp.dot(
        left_q, residual, precision=HIGHEST_PRECISION, preferred_element_type=jnp.float32
    )
    middle = jnp.dot(
        middle, right_q.T, precision=HIGHEST_PRECISION, preferred_element_type=jnp.float32
    )
    middle = middle / (left_e[:, None] + right_e[None, :])
    product = jnp.dot(
        left_p, middle, precision=HIGHEST_PRECISION, preferred_element_type=jnp.float32
    )
    return -jnp.dot(
        product, right_p.T, precision=HIGHEST_PRECISION, preferred_element_type=jnp.float32
    )


def pick_slot(stacked, slot_index):
    return lax.dynamic_index_in_dim(stacked, slot_index, 0, keepdims=False)


def on_device(state, coupling, coupling_t, factor, cofactor, rates):
    row_count = lax.axis_size("row")
    col_count = lax.axis_size("col")
    half_rows = row_count // 2
    order_blocks = 2 * row_count
    col_slots = order_blocks // col_count
    block_size = state.shape[0]
    row_index = lax.axis_index("row")
    col_index = lax.axis_index("col")
    blocks = jnp.transpose(state.reshape(block_size, col_slots, block_size), (1, 0, 2))
    full_p, full_q = (
        lax.all_gather(factor, "row", axis=2, tiled=True),
        lax.all_gather(cofactor, "row", axis=2, tiled=True),
    )
    right_ps = full_p.reshape(col_slots, block_size, block_size)
    right_qs = full_q.reshape(col_slots, block_size, block_size)
    right_es = rates.reshape(col_slots, block_size)
    own_slot = row_index // col_count
    picked = (
        pick_slot(right_ps, own_slot),
        pick_slot(right_qs, own_slot),
        pick_slot(right_es, own_slot),
    )
    left_p, left_q, left_e = (
        broadcast(picked[0], "col", row_index % col_count),
        broadcast(picked[1], "col", row_index % col_count),
        broadcast(picked[2], "col", row_index % col_count),
    )
    upper_row = coupling.reshape(block_size, col_slots * block_size)
    lower_pair = coupling_t.reshape(2, block_size, col_slots * block_size)
    my_columns = col_index + col_count * jnp.arange(col_slots, dtype=jnp.int32)
    upper_now = upper_row
    for wave_step in range(STEPS):
        antidiag = order_blocks - 1 - wave_step
        partner = antidiag - row_index
        owner_col = partner % col_count
        slot_here = partner // col_count
        usable = row_index <= partner
        residual = pick_slot(blocks, slot_here)
        solution = solve_block(
            residual,
            left_p,
            left_q,
            left_e,
            pick_slot(right_ps, slot_here),
            pick_slot(right_qs, slot_here),
            pick_slot(right_es, slot_here),
        )
        solution = jnp.where(usable, solution, 0.0)
        written = jnp.where(usable & (col_index == owner_col), solution, residual)
        blocks = lax.dynamic_update_index_in_dim(blocks, written, slot_here, 0)
        shared = broadcast(solution, "col", owner_col)
        mirror = antidiag - my_columns
        use_row = mirror <= my_columns
        sources = jnp.clip(jnp.where(use_row, mirror, my_columns), 0, row_count - 1)
        offered = jnp.where((sources == row_index)[:, None, None], shared[None], 0.0)
        fetched = lax.psum(offered, "row")
        partner_blocks = jnp.where(use_row[:, None, None], fetched, jnp.swapaxes(fetched, 1, 2))
        if wave_step > 0:
            upper_now = from_behind(upper_row, "col", (col_count - wave_step) % col_count)
        receiver = (row_index - wave_step - half_rows) % row_count
        send_slot = jnp.where(receiver + wave_step >= row_count, 1, 0)
        send_piece = pick_slot(lower_pair, send_slot)
        lower_now = from_behind(send_piece, "row", (half_rows - wave_step) % row_count)
        upper_view = upper_now.reshape(block_size, col_slots, block_size)
        rolled = jnp.where(
            (col_index + wave_step) // col_count == 1, jnp.roll(upper_view, -1, axis=1), upper_view
        )
        lower_view = lower_now.reshape(block_size, col_slots, block_size)
        left_terms = jnp.einsum(
            "aub,ubc->uac", rolled.astype(jnp.float32), partner_blocks, precision=HIGHEST_PRECISION
        )
        right_terms = jnp.einsum(
            "ab,buc->uac", shared, lower_view.astype(jnp.float32), precision=HIGHEST_PRECISION
        )
        targets = (row_index <= my_columns) & (row_index + my_columns < antidiag)
        blocks = blocks - jnp.where(targets[:, None, None], left_terms + right_terms, 0.0)
    return jnp.transpose(blocks, (1, 0, 2)).reshape(block_size, 1, col_slots * block_size)


def solution(mesh):
    return jax.shard_map(
        on_device,
        mesh=mesh,
        in_specs=(
            P("row", "col", None),
            P("row", "col", None),
            P(None, "row", "col", None),
            P(None, "col", "row", None),
            P(None, "col", "row", None),
            P(None, "col", None),
        ),
        out_specs=P("row", "col", None),
        check_vma=False,
    )
```

profile of v0, /device:TPU:0, one launch (start us, length us, event | category | flops | bytes accessed | tf_op | source)
XLA Modules:
  0.0 328.6 jit_solution(1007737203448546680)
XLA Ops:
  6.5 0.7 all-gather.3.cloned.1.call-update
  7.3 0.0 all-gather.5.cloned.1.call-start
  7.3 0.7 all-gather.5.cloned.1.call-update
  8.0 0.0 all-reduce.15.cloned.1.call-start
  8.1 27.3 %all-gather.3.cloned.1.call-done = f32[4,1,256,256]{3,2,1,0:T(8,128)} async-done(((f32[4,1,32,256]{3,2,1,0:T(8,128)}), f32[4,1,256,256]{3,2,1,0:T(8,128)}) %all-gather.3.cloned.1.call-update) | async-done | bytes 1048592 | tf_op jit(solution)/shard_map/all_gather | solution.py:52
  35.4 1.7 select_bitcast_fusion.1
  37.0 23.6 %all-gather.5.cloned.1.call-done = f32[4,1,256,256]{3,2,1,0:T(8,128)} async-done(((f32[4,1,32,256]{3,2,1,0:T(8,128)}), f32[4,1,256,256]{3,2,1,0:T(8,128)}) %all-gather.5.cloned.1.call-update) | async-done | bytes 1048592 | tf_op jit(solution)/shard_map/all_gather | solution.py:53
  60.7 1.7 select_bitcast_fusion
  62.3 0.0 all-reduce.15.cloned.1.call-update
  62.4 0.0 all-reduce.7.cloned.1.call-start
  62.4 1.0 copy.19
  63.4 0.1 copy.51
  63.5 0.0 copy-start.15
  63.5 0.7 copy-done.15
  64.2 11.9 %psum.51 = f32[256]{0:T(256)S(1)} all-reduce(f32[256]{0:T(256)S(1)} %bitcast.106), channel_id=1, replica_groups=mesh['row'=8,'col'=4] {'col'}, use_global_device_ids=true, to_apply=%region_2.3 | all-reduce | flops 256 | bytes 2048 | tf_op jit(solution)/shard_map/psum | solution.py:12
  76.1 25.7 %all-reduce.15.cloned.1.call-done = (f32[256,256]{1,0:T(8,128)}, f32[256,256]{1,0:T(8,128)}) async-done(((f32[256,256]{1,0:T(8,128)}, f32[256,256]{1,0:T(8,128)}), (f32[256,256]{1,0:T(8,128)}, f32[256,256]{1,0:T(8,128)})) %all-reduce.15.cloned.1.call-update) | async-done | bytes 524304 | tf_op jit(solution)/shard_map/psum | solution.py:12
  101.8 1.4 fusion.24
  103.2 1.4 convolution_divide_fusion.1
  104.6 0.4 fusion.45
  105.0 0.0 copy-start.10
  105.0 1.5 bitcast_dynamic-update-slice_fusion.1
  106.5 0.0 copy-start.2
  106.5 0.8 broadcast_select_fusion.3
  107.3 0.0 all-reduce.7.cloned.1.call-update
  107.3 0.0 all-reduce.9.cloned.1.call-start
  107.4 1.1 dynamic-slice_bitcast_fusion
  108.5 1.5 collective-permute-start
  110.0 32.9 %all-reduce.7.cloned.1.call-done = f32[256,256]{0,1:T(8,128)} async-done(((f32[256,256]{0,1:T(8,128)}), f32[256,256]{0,1:T(8,128)}) %all-reduce.7.cloned.1.call-update) | async-done | bytes 262160 | tf_op jit(solution)/shard_map/psum | solution.py:12
  142.9 2.1 broadcast_select_fusion.1
  145.0 0.0 all-reduce.9.cloned.1.call-update
  145.0 0.0 all-reduce.11.cloned.1.call-start
  145.0 1.0 copy-done.12
  146.0 0.4 reshape_reshape.3
  146.4 0.2 slice.19
  146.6 0.3 slice.18
  146.9 0.7 copy.46
  147.5 0.1 copy.47
  147.7 0.2 copy.24
  147.9 54.7 %all-reduce.9.cloned.1.call-done = f32[4,256,256]{1,2,0:T(8,128)} async-done(((f32[4,256,256]{1,2,0:T(8,128)}), f32[4,256,256]{1,2,0:T(8,128)}) %all-reduce.9.cloned.1.call-update) | async-done | bytes 1048592 | tf_op jit(solution)/shard_map/psum | solution.py:97
  202.5 1.6 copy.23
  204.2 1.7 fusion.7
  206.0 0.6 fusion.4
  206.7 0.9 copy-done.11
  207.6 0.4 fusion.19
  208.0 1.4 convolution_divide_fusion
  209.4 0.4 fusion.46
  209.8 1.4 bitcast_dynamic-update-slice_fusion
  211.3 0.7 broadcast_select_fusion.2
  212.0 0.0 all-reduce.11.cloned.1.call-update
  212.0 0.0 all-reduce.13.cloned.1.call-start
  212.1 0.1 collective-permute-start.2
  212.2 0.3 copy-done.13
  212.4 3.3 collective-permute-start.1
  215.7 36.9 %all-reduce.11.cloned.1.call-done = f32[256,256]{0,1:T(8,128)} async-done(((f32[256,256]{0,1:T(8,128)}), f32[256,256]{0,1:T(8,128)}) %all-reduce.11.cloned.1.call-update) | async-done | bytes 262160 | tf_op jit(solution)/shard_map/psum | solution.py:12
  252.6 2.1 broadcast_select_fusion
  254.7 0.0 all-reduce.13.cloned.1.call-update
  254.8 0.8 copy-done.4
  255.5 0.6 slice.21
  256.2 1.3 copy.30
  257.5 0.6 convolution_bitcast_fusion
  258.1 54.2 %all-reduce.13.cloned.1.call-done = f32[4,256,256]{1,2,0:T(8,128)} async-done(((f32[4,256,256]{1,2,0:T(8,128)}), f32[4,256,256]{1,2,0:T(8,128)}) %all-reduce.13.cloned.1.call-update) | async-done | bytes 1048592 | tf_op jit(solution)/shard_map/psum | solution.py:97
  312.4 2.6 copy.29
  315.0 3.2 fusion.1
  318.2 3.6 %copy.32 = f32[256,1,1024]{2,1,0:T(1,128)} copy(f32[256,1,1024]{0,2,1:T(8,128)} %bitcast.98) | data formatting | bytes 2097152 | tf_op jit(solution)/shard_map/reshape | solution.py:118
  (37 shorter events, 0.2 us)
Async XLA Ops:
  6.5 55.9 %copy-start.9 = (f32[256,1,1024]{2,1,0:T(1,128)S(1)}, f32[256,1,1024]{2,1,0:T(1,128)}, u32[]{:S(2)}) copy-start(f32[256,1,1024]{2,1,0:T(1,128)} %param.6) | copy-start | bytes 3145732
  6.5 28.8 %all-gather.3.cloned.1.call-start = ((), (), s32[]{:S(2)}) async-start(), calls=%async_computation | async-start | bytes 1179648 | tf_op jit(solution)/shard_map/all_gather | solution.py:52
  7.3 53.4 %all-gather.5.cloned.1.call-start = ((), (), s32[]{:S(2)}) async-start(), calls=%async_computation.1 | async-start | bytes 1179648 | tf_op jit(solution)/shard_map/all_gather | solution.py:53
  8.0 93.8 %all-reduce.15.cloned.1.call-start = ((), (), s32[]{:S(2)}) async-start(), calls=%async_computation.6 | async-start | bytes 1048576 | tf_op jit(solution)/shard_map/psum | solution.py:12
  62.4 80.6 %all-reduce.7.cloned.1.call-start = ((), (), s32[]{:S(2)}) async-start(), calls=%async_computation.2 | async-start | bytes 524288 | tf_op jit(solution)/shard_map/psum | solution.py:12
  63.5 0.7 copy-start.15
  103.2 1.4 copy-start.5
  105.0 2.4 copy-start.10
  106.5 2.0 copy-start.2
  107.3 95.2 %all-reduce.9.cloned.1.call-start = ((), (), s32[]{:S(2)}) async-start(), calls=%async_computation.3 | async-start | bytes 2097152 | tf_op jit(solution)/shard_map/psum | solution.py:97
  108.5 39.2 %collective-permute-start = (bf16[256,1024]{1,0:T(8,128)(2,1)}, bf16[256,1024]{1,0:T(8,128)(2,1)S(1)}, u32[]{:S(2)}, u32[]{:S(2)}) collective-permute-start(bf16[256,1024]{1,0:T(8,128)(2,1)} %get-tuple-element.8), channel_id=1, source_target_pairs={{16,0},{20,4},{24,8},{28,12},{0,16},{4,20},{8,24},{12,28},{17,1},{... | collective-permute-start | bytes 1572872 | tf_op jit(solution)/shard_map/ppermute | solution.py:18
  145.0 1.0 copy-start.12
  145.0 107.6 %all-reduce.11.cloned.1.call-start = ((), (), s32[]{:S(2)}) async-start(), calls=%async_computation.4 | async-start | bytes 524288 | tf_op jit(solution)/shard_map/psum | solution.py:12
  202.5 1.7 copy-start
  204.2 1.8 copy-start.3
  204.2 1.8 copy-start.7
  206.6 1.0 copy-start.11
  208.0 1.4 copy-start.6
  209.8 2.3 copy-start.14
  211.3 1.1 copy-start.13
  212.0 100.3 %all-reduce.13.cloned.1.call-start = ((), (), s32[]{:S(2)}) async-start(), calls=%async_computation.5 | async-start | bytes 2097152 | tf_op jit(solution)/shard_map/psum | solution.py:97
  212.1 44.1 %collective-permute-start.2 = (bf16[256,1024]{1,0:T(8,128)(2,1)S(1)}, bf16[256,1024]{1,0:T(8,128)(2,1)}, u32[]{:S(2)}, u32[]{:S(2)}) collective-permute-start(bf16[256,1024]{1,0:T(8,128)(2,1)S(1)} %copy-done.14), channel_id=1, source_target_pairs={{20,0},{24,4},{28,8},{0,12},{4,16},{8,20},{12,24},{16,28},{21,1},{... | collective-permute-start | bytes 1572872 | tf_op jit(solution)/shard_map/ppermute | solution.py:18
  212.4 42.3 %collective-permute-start.1 = (bf16[256,1024]{1,0:T(8,128)(2,1)S(1)}, bf16[256,1024]{1,0:T(8,128)(2,1)S(1)}, u32[]{:S(2)}, u32[]{:S(2)}) collective-permute-start(bf16[256,1024]{1,0:T(8,128)(2,1)S(1)} %bitcast.105), channel_id=1, source_target_pairs={{1,0},{2,1},{3,2},{0,3},{5,4},{6,5},{7,6},{4,7},{9,8},{10,9},{11,1... | collective-permute-start | bytes 1572872 | tf_op jit(solution)/shard_map/ppermute | solution.py:18
  254.7 0.8 copy-start.4
  256.2 1.3 copy-start.8
  312.4 2.6 copy-start.1
Sparse Core Ops, SparseCore 0:
  9.2 26.0 all-gather.2
  37.3 23.3 all-gather.4
  63.1 38.7 all-reduce.14
  107.4 35.4 all-reduce.6
  145.9 56.5 all-reduce.8
  212.2 40.3 all-reduce.10
  255.7 56.5 all-reduce.12
where the time goes:
time: 329 us
  waiting for transfers between devices  257 us (78%)
  local copies, waits for them, and re-layouts  17.3 us (5%)
  matrix products  14.4 us (4%)
  between operations  14 us (4%)
  blocking collectives  11.9 us (4%)
  other arithmetic  9.03 us (3%)
  starting transfers between devices  5.04 us (2%)
    psum x2, waiting for transfers between devices, on_device(): fetched = lax.psum(offered, 'row')  109 us
    psum x3, waiting for transfers between devices, broadcast(): return lax.psum(block, axis)  95.5 us
    all_gather x1, waiting for transfers between devices, on_device(): lax.all_gather(factor, 'row', axis=2, tiled=True)  27.3 us
    all_gather x1, waiting for transfers between devices, on_device(): lax.all_gather(cofactor, 'row', axis=2, tiled=True)  23.6 us
    psum x1, blocking collectives, broadcast(): return lax.psum(block, axis)  11.9 us
  transfers between devices with their start and end apart: 10, of which 7 were waited for; matrix products, arithmetic and copies ran while one was open for 4% of the time, Pallas kernels for 0%

commit v1 on v0

--- a/solution.py
+++ b/solution.py
@@ -5,6 +5,9 @@
 
 STEPS = 2
 HIGHEST_PRECISION = lax.Precision.HIGHEST
+finish_page = lambda in_array, dim_no: jnp.concatenate(
+    jax.lax.all_gather(in_array, axis_name="row"), axis=dim_no
+)
 
 
 def broadcast(block, axis, source):
@@ -48,10 +51,7 @@
     row_index = lax.axis_index("row")
     col_index = lax.axis_index("col")
     blocks = jnp.transpose(state.reshape(block_size, col_slots, block_size), (1, 0, 2))
-    full_p, full_q = (
-        lax.all_gather(factor, "row", axis=2, tiled=True),
-        lax.all_gather(cofactor, "row", axis=2, tiled=True),
-    )
+    full_p, full_q = (lax.all_gather(factor, "row", axis=2, tiled=True), finish_page(cofactor, 2))
     right_ps = full_p.reshape(col_slots, block_size, block_size)
     right_qs = full_q.reshape(col_slots, block_size, block_size)
     right_es = rates.reshape(col_slots, block_size)

time: 329 us -> 329 us (level)
    all_gather x1, waiting for transfers between devices: 27.3 us -> 23.2 us  [on_device(): lax.all_gather(factor, 'row', axis=2, tiled=True)]
    all_gather x1, waiting for transfers between devices: 23.6 us -> 27.3 us  [jax.lax.all_gather(in_array, axis_name='row')]
where the time goes in v1:
time: 329 us; the launch traced here: 328 us
  waiting for transfers between devices  256 us (78%)
  local copies, waits for them, and re-layouts  19.2 us (6%)
  between operations  14.1 us (4%)
  matrix products  13.4 us (4%)
  blocking collectives  11.9 us (4%)
  other arithmetic  8.09 us (2%)
  starting transfers between devices  5.04 us (2%)
    psum x2, waiting for transfers between devices, on_device(): fetched = lax.psum(offered, 'row')  109 us
    psum x3, waiting for transfers between devices, broadcast(): return lax.psum(block, axis)  95.5 us
    all_gather x1, waiting for transfers between devices, jax.lax.all_gather(in_array, axis_name='row')  27.3 us
    all_gather x1, waiting for transfers between devices, on_device(): lax.all_gather(factor, 'row', axis=2, tiled=True)  23.2 us
    psum x1, blocking collectives, broadcast(): return lax.psum(block, axis)  11.9 us
  transfers between devices with their start and end apart: 10, of which 7 were waited for; matrix products, arithmetic and copies ran while one was open for 4% of the time, Pallas kernels for 0%

profile of v1, /device:TPU:0, one launch (start us, length us, event | category | flops | bytes accessed | tf_op | source)
XLA Modules:
  0.0 328.1 jit_solution(14976392365234482496)
XLA Ops:
  6.5 0.7 all-gather.6.cloned.1.call-update
  7.3 0.0 all-gather.4.cloned.1.call-start
  7.3 0.7 all-gather.4.cloned.1.call-update
  8.0 0.0 all-reduce.15.cloned.1.call-start
  8.1 27.3 %all-gather.6.cloned.1.call-done = f32[32,1,32,256]{3,2,1,0:T(8,128)} async-done(((f32[4,1,32,256]{3,2,1,0:T(8,128)}), f32[32,1,32,256]{3,2,1,0:T(8,128)}) %all-gather.6.cloned.1.call-update) | async-done | bytes 1048592 | tf_op jit(solution)/shard_map/all_gather | solution.py:9
  35.3 1.3 copy.50
  36.7 0.7 select_bitcast_fusion
  37.4 23.2 %all-gather.4.cloned.1.call-done = f32[4,1,256,256]{3,2,1,0:T(8,128)} async-done(((f32[4,1,32,256]{3,2,1,0:T(8,128)}), f32[4,1,256,256]{3,2,1,0:T(8,128)}) %all-gather.4.cloned.1.call-update) | async-done | bytes 1048592 | tf_op jit(solution)/shard_map/all_gather | solution.py:54
  60.7 1.7 select_bitcast_fusion.1
  62.3 0.0 all-reduce.15.cloned.1.call-update
  62.3 0.0 all-reduce.7.cloned.1.call-start
  62.4 1.0 copy.49
  63.4 0.1 copy.82
  63.5 0.7 copy-done.16
  64.2 11.9 %psum.51 = f32[256]{0:T(256)S(1)} all-reduce(f32[256]{0:T(256)S(1)} %bitcast.114), channel_id=1, replica_groups=mesh['row'=8,'col'=4] {'col'}, use_global_device_ids=true, to_apply=%region_2.3 | all-reduce | flops 256 | bytes 2048 | tf_op jit(solution)/shard_map/psum | solution.py:15
  76.1 25.7 %all-reduce.15.cloned.1.call-done = (f32[256,256]{1,0:T(8,128)}, f32[256,256]{1,0:T(8,128)}) async-done(((f32[256,256]{1,0:T(8,128)}, f32[256,256]{1,0:T(8,128)}), (f32[256,256]{1,0:T(8,128)}, f32[256,256]{1,0:T(8,128)})) %all-reduce.15.cloned.1.call-update) | async-done | bytes 524304 | tf_op jit(solution)/shard_map/psum | solution.py:15
  101.8 1.4 fusion.24
  103.2 0.4 convolution_divide_fusion.1
  103.6 0.5 copy-done.6
  104.1 0.4 fusion.45
  104.5 1.5 bitcast_dynamic-update-slice_fusion.1
  106.0 0.0 copy-start.2
  106.0 0.8 broadcast_select_fusion.3
  106.8 0.0 all-reduce.7.cloned.1.call-update
  106.8 0.0 all-reduce.9.cloned.1.call-start
  106.9 1.1 dynamic-slice_bitcast_fusion
  108.0 1.5 collective-permute-start
  109.5 32.9 %all-reduce.7.cloned.1.call-done = f32[256,256]{0,1:T(8,128)} async-done(((f32[256,256]{0,1:T(8,128)}), f32[256,256]{0,1:T(8,128)}) %all-reduce.7.cloned.1.call-update) | async-done | bytes 262160 | tf_op jit(solution)/shard_map/psum | solution.py:15
  142.4 2.1 broadcast_select_fusion.1
  144.5 0.0 all-reduce.9.cloned.1.call-update
  144.5 0.0 all-reduce.11.cloned.1.call-start
  144.5 1.0 copy-done.13
  145.5 0.4 reshape_reshape.7
  145.9 0.2 slice.19
  146.1 0.3 slice.18
  146.4 0.7 copy.77
  147.0 0.1 copy.78
  147.2 0.2 copy.55
  147.4 54.7 %all-reduce.9.cloned.1.call-done = f32[4,256,256]{1,2,0:T(8,128)} async-done(((f32[4,256,256]{1,2,0:T(8,128)}), f32[4,256,256]{1,2,0:T(8,128)}) %all-reduce.9.cloned.1.call-update) | async-done | bytes 1048592 | tf_op jit(solution)/shard_map/psum | solution.py:97
  202.0 1.6 copy.54
  203.7 1.7 fusion.7
  205.5 0.6 fusion.4
  206.2 0.9 copy-done.12
  207.1 0.4 fusion.19
  207.5 1.4 convolution_divide_fusion
  208.9 0.4 fusion.46
  209.3 1.4 bitcast_dynamic-update-slice_fusion
  210.8 0.7 broadcast_select_fusion.2
  211.5 0.0 all-reduce.11.cloned.1.call-update
  211.5 0.0 all-reduce.13.cloned.1.call-start
  211.6 0.1 collective-permute-start.2
  211.7 0.3 copy-done.14
  211.9 3.3 collective-permute-start.1
  215.2 36.9 %all-reduce.11.cloned.1.call-done = f32[256,256]{0,1:T(8,128)} async-done(((f32[256,256]{0,1:T(8,128)}), f32[256,256]{0,1:T(8,128)}) %all-reduce.11.cloned.1.call-update) | async-done | bytes 262160 | tf_op jit(solution)/shard_map/psum | solution.py:15
  252.1 2.1 broadcast_select_fusion
  254.1 0.0 all-reduce.13.cloned.1.call-update
  254.3 0.8 copy-done.4
  255.0 0.7 slice.21
  255.7 1.3 copy.61
  257.0 0.6 convolution_bitcast_fusion
  257.6 54.2 %all-reduce.13.cloned.1.call-done = f32[4,256,256]{1,2,0:T(8,128)} async-done(((f32[4,256,256]{1,2,0:T(8,128)}), f32[4,256,256]{1,2,0:T(8,128)}) %all-reduce.13.cloned.1.call-update) | async-done | bytes 1048592 | tf_op jit(solution)/shard_map/psum | solution.py:97
  311.8 2.6 copy.60
  314.5 3.2 fusion.1
  317.6 3.6 %copy.63 = f32[256,1,1024]{2,1,0:T(1,128)} copy(f32[256,1,1024]{0,2,1:T(8,128)} %bitcast.102) | data formatting | bytes 2097152 | tf_op jit(solution)/shard_map/reshape | solution.py:118
  (40 shorter events, 0.2 us)
Async XLA Ops:
  6.5 28.8 %all-gather.6.cloned.1.call-start = ((), (), s32[]{:S(2)}) async-start(), calls=%async_computation.5 | async-start | bytes 1179648 | tf_op jit(solution)/shard_map/all_gather | solution.py:9
  7.3 53.4 %all-gather.4.cloned.1.call-start = ((), (), s32[]{:S(2)}) async-start(), calls=%async_computation | async-start | bytes 1179648 | tf_op jit(solution)/shard_map/all_gather | solution.py:54
  8.0 93.8 %all-reduce.15.cloned.1.call-start = ((), (), s32[]{:S(2)}) async-start(), calls=%async_computation.6 | async-start | bytes 1048576 | tf_op jit(solution)/shard_map/psum | solution.py:15
  36.7 66.5 %copy-start.5 = (f32[4,1,8,32,256]{4,3,2,0,1:T(8,128)}, f32[4,1,8,32,256]{4,3,2,0,1:T(8,128)S(1)}, u32[]{:S(2)}) copy-start(f32[4,1,8,32,256]{4,3,2,0,1:T(8,128)S(1)} %copy.50) | copy-start | bytes 3145732
  36.7 25.8 %copy-start.10 = (f32[256,1,1024]{2,1,0:T(1,128)S(1)}, f32[256,1,1024]{2,1,0:T(1,128)}, u32[]{:S(2)}) copy-start(f32[256,1,1024]{2,1,0:T(1,128)} %param.6) | copy-start | bytes 3145732
  62.3 80.1 %all-reduce.7.cloned.1.call-start = ((), (), s32[]{:S(2)}) async-start(), calls=%async_computation.1 | async-start | bytes 524288 | tf_op jit(solution)/shard_map/psum | solution.py:15
  63.5 0.7 copy-start.16
  103.2 1.0 copy-start.6
  104.5 2.4 copy-start.11
  106.0 2.0 copy-start.2
  106.8 95.2 %all-reduce.9.cloned.1.call-start = ((), (), s32[]{:S(2)}) async-start(), calls=%async_computation.2 | async-start | bytes 2097152 | tf_op jit(solution)/shard_map/psum | solution.py:97
  108.0 39.2 %collective-permute-start = (bf16[256,1024]{1,0:T(8,128)(2,1)}, bf16[256,1024]{1,0:T(8,128)(2,1)S(1)}, u32[]{:S(2)}, u32[]{:S(2)}) collective-permute-start(bf16[256,1024]{1,0:T(8,128)(2,1)} %get-tuple-element.8), channel_id=1, source_target_pairs={{16,0},{20,4},{24,8},{28,12},{0,16},{4,20},{8,24},{12,28},{17,1},{... | collective-permute-start | bytes 1572872 | tf_op jit(solution)/shard_map/ppermute | solution.py:21
  144.5 1.0 copy-start.13
  144.5 107.6 %all-reduce.11.cloned.1.call-start = ((), (), s32[]{:S(2)}) async-start(), calls=%async_computation.3 | async-start | bytes 524288 | tf_op jit(solution)/shard_map/psum | solution.py:15
  202.0 1.7 copy-start
  203.7 1.8 copy-start.3
  203.7 1.8 copy-start.8
  206.1 1.0 copy-start.12
  207.5 1.4 copy-start.7
  209.3 2.3 copy-start.15
  210.8 1.1 copy-start.14
  211.5 100.3 %all-reduce.13.cloned.1.call-start = ((), (), s32[]{:S(2)}) async-start(), calls=%async_computation.4 | async-start | bytes 2097152 | tf_op jit(solution)/shard_map/psum | solution.py:97
  211.6 44.1 %collective-permute-start.2 = (bf16[256,1024]{1,0:T(8,128)(2,1)S(1)}, bf16[256,1024]{1,0:T(8,128)(2,1)}, u32[]{:S(2)}, u32[]{:S(2)}) collective-permute-start(bf16[256,1024]{1,0:T(8,128)(2,1)S(1)} %copy-done.15), channel_id=1, source_target_pairs={{20,0},{24,4},{28,8},{0,12},{4,16},{8,20},{12,24},{16,28},{21,1},{... | collective-permute-start | bytes 1572872 | tf_op jit(solution)/shard_map/ppermute | solution.py:21
  211.9 42.3 %collective-permute-start.1 = (bf16[256,1024]{1,0:T(8,128)(2,1)S(1)}, bf16[256,1024]{1,0:T(8,128)(2,1)S(1)}, u32[]{:S(2)}, u32[]{:S(2)}) collective-permute-start(bf16[256,1024]{1,0:T(8,128)(2,1)S(1)} %bitcast.113), channel_id=1, source_target_pairs={{1,0},{2,1},{3,2},{0,3},{5,4},{6,5},{7,6},{4,7},{9,8},{10,9},{11,1... | collective-permute-start | bytes 1572872 | tf_op jit(solution)/shard_map/ppermute | solution.py:21
  254.2 0.8 copy-start.4
  255.7 1.3 copy-start.9
  311.8 2.6 copy-start.1
Sparse Core Ops, SparseCore 0:
  9.2 26.0 all-gather.5
  37.2 23.3 all-gather.3
  63.0 38.7 all-reduce.14
  106.9 35.4 all-reduce.6
  145.4 56.5 all-reduce.8
  211.6 40.3 all-reduce.10
  255.2 56.5 all-reduce.12
